TPU v7x, 32 devices: a whole 2x2x4 slice. The times are simulated.
32 devices in a mesh: grp: 2 (over y), row: 4 (over z), col: 4 (over x, core).
Axes of the slice: x: 2, y: 2, z: 4, core: 2. Of those that a mesh axis runs over, the one named last changes fastest.
Arguments:
- z_spectra: float32 [32, 2, 2, 4096], P(('grp', 'row', 'col')), parts along dimension 0, may hold values from -6 to 6
- n_spectra: float32 [32, 2, 2, 4096], P(('grp', 'col', 'row')), parts along dimension 0, may hold values from -6 to 6
- z_flags: int32 [32, 2], P(('grp', 'row', 'col')), parts along dimension 0, may hold values 0 or 1
- n_flags: int32 [32, 2], P(('grp', 'col', 'row')), parts along dimension 0, may hold values 0 or 1
- pair_mask: int32 [32, 16], P(('grp', 'row'), 'col'), parts along dimension 0, may hold values 0 or 1
Outputs:
- stacks: float32 [32, 16, 512], P(('grp', 'row'), 'col'), parts along dimension 0
There are 2 independent parts, one for each index of `grp`. A program takes and returns all parts, laid end to end along the dimension named above; each array names one. Nothing has to cross between parts.
All inputs are finite; a program needn't handle non-finite values. No bound on the sum of `z_flags` or of `n_flags` or of `pair_mask` on one device may be relied on, other than what follows from the above.
Results may differ from a plain program's by a relative error of at most 0.0037.
Values sent between devices are 32-bit elements; how exact they have to be, the bound alone decides.
No kernel may reach another device: no remote copies, remote signals or barrier semaphores. Data moves between devices by JAX's collectives and lax.ppermute only.
A program may use at most 64 MiB of HBM per device.

v0:
```python
import math

import jax
import jax.numpy as jnp
from jax import lax
from jax.sharding import PartitionSpec as P

F = 4096
LAGS = 512
BANDS = 8


def lag_table(bin_count, total_bins, lag_count):
    freq_bins = jnp.arange(bin_count, dtype=jnp.int32)
    lag_steps = jnp.arange(lag_count, dtype=jnp.int32) - lag_count // 2
    phase_index = freq_bins[:, None] * lag_steps[None, :] % (2 * total_bins)
    angles = phase_index.astype(jnp.float32) * (math.pi / total_bins)
    weight = jnp.where(freq_bins == 0, 1.0, 2.0).astype(jnp.float32)[:, None]
    return jnp.concatenate([weight * jnp.cos(angles), -weight * jnp.sin(angles)], 0).astype(
        jnp.bfloat16
    )


def band_rows(full_table, first_bin, band_width, total_bins):
    real_rows = lax.dynamic_slice_in_dim(full_table, first_bin, band_width, 0)
    imag_rows = lax.dynamic_slice_in_dim(full_table, total_bins + first_bin, band_width, 0)
    return jnp.concatenate([real_rows, imag_rows], 0)


def correlate(row_spec, col_spec, lag_tab):
    z_real = row_spec[:, None, :, 0, :]
    z_imag = row_spec[:, None, :, 1, :]
    n_real = col_spec[None, :, :, 0, :]
    n_imag = col_spec[None, :, :, 1, :]
    real_part = z_real * n_real + z_imag * n_imag
    imag_part = z_imag * n_real - z_real * n_imag
    row_count, col_count, windows, bins = real_part.shape
    cross_spec = jnp.stack([real_part, imag_part], 3).astype(jnp.bfloat16)
    merged = cross_spec.reshape(row_count * col_count * windows, 2 * bins)
    product = jnp.dot(merged, lag_tab, preferred_element_type=jnp.float32)
    return product.reshape(row_count, col_count, windows, lag_tab.shape[1])


def stack_windows(corr, pair_marks):
    spread = jnp.sqrt(jnp.mean(corr * corr, -1, keepdims=True) + 1e-05)
    unit_corr = corr / spread
    window_count = jnp.maximum(jnp.sum(pair_marks, -1), 1.0)
    summed = jnp.sum(pair_marks[..., None] * unit_corr, -2)
    return summed / window_count[..., None]


def body(z_spectra, n_spectra, z_flags, n_flags, pair_mask):
    z_rows, z_marks = (
        lax.all_gather(z_spectra, "col", axis=0, tiled=True),
        lax.all_gather(z_flags.astype(jnp.float32), "col", axis=0, tiled=True),
    )
    n_marks = n_flags.astype(jnp.float32)
    row_count = z_rows.shape[0]
    windows = z_spectra.shape[1]
    band_width = F // BANDS
    full_table = lag_table(F, F, LAGS)
    col_spec = lax.all_gather(n_spectra, "row", axis=0, tiled=True)
    piece_marks = lax.all_gather(n_marks, "row", axis=0, tiled=True)

    def add_band(band_index, summed):
        first_bin = band_index * band_width
        lag_tab = band_rows(full_table, first_bin, band_width, F)
        z_band = lax.dynamic_slice_in_dim(z_rows, first_bin, band_width, 3)
        n_band = lax.dynamic_slice_in_dim(col_spec, first_bin, band_width, 3)
        return summed + correlate(z_band, n_band, lag_tab)

    initial = jnp.zeros((row_count, col_spec.shape[0], windows, LAGS), jnp.float32)
    corr = lax.fori_loop(0, BANDS, add_band, initial)
    running = corr
    joined = z_marks[:, None, :] * piece_marks[None, :, :]
    marks_now = joined
    state = (running, marks_now)
    running, marks_now = state
    stacked = stack_windows(running, marks_now)
    return stacked * pair_mask.astype(jnp.float32)[..., None]


def solution(mesh):
    placed = (
        P(("grp", "row", "col"), None, None, None),
        P(("grp", "col", "row"), None, None, None),
        P(("grp", "row", "col"), None),
        P(("grp", "col", "row"), None),
        P(("grp", "row"), "col"),
    )
    return jax.shard_map(
        body, mesh=mesh, in_specs=placed, out_specs=P(("grp", "row"), "col", None), check_vma=False
    )
```

profile of v0, /device:TPU:0, one launch (start us, length us, event | category | flops | bytes accessed | tf_op | source)
XLA Modules:
  0.0 99.7 jit_solution(9673217633503370301)
XLA Ops:
  0.0 36.3 %multiply_convert_fusion.1 = (bf16[4096,512]{1,0:T(8,128)(2,1)}, bf16[4096,512]{1,0:T(8,128)(2,1)}) fusion(s32[512]{0:T(512)S(1)} %iota_add_fusion, f32[4096]{0:T(1024)S(1)} %get-tuple-element.185, f32[4096]{0:T(1024)S(1)} %get-tuple-element.186), kind=kLoop, calls=%fused_computation.24 | loop fusion | flops 37748736 | bytes 8423424 | tf_op jit(solution)/shard_map/convert.2
  36.3 7.3 %pad_maximum_fusion.1 = bf16[8192,512]{1,0:T(8,128)(2,1)} fusion(bf16[4096,512]{1,0:T(8,128)(2,1)} %get-tuple-element.184, bf16[4096,512]{1,0:T(8,128)(2,1)} %get-tuple-element.183), kind=kLoop, calls=%fused_computation.22 | loop fusion | flops 16777216 | bytes 16777216 | tf_op jit(solution)/shard_map/concatenate | solution.py:19
  43.6 7.2 %all_gather.14 = f32[4,2,2,4096]{3,1,0,2:T(2,128)S(1)} all-gather(f32[1,2,2,4096]{3,1,0,2:T(2,128)S(1)} %copy.14), channel_id=1, replica_groups=mesh['grp'=2,'row'=4,'col'=4] {'col'}, dimensions={0}, use_global_device_ids=true | all-gather | bytes 327680 | tf_op jit(solution)/shard_map/all_gather | solution.py:54
  50.8 14.1 %all_gather.15 = f32[4,2,2,4096]{3,2,1,0:T(2,128)S(1)} all-gather(f32[1,2,2,4096]{3,2,1,0:T(2,128)S(1)} %copy-done), channel_id=1, replica_groups=mesh['grp'=2,'row'=4,'col'=4] {'row'}, dimensions={0}, use_global_device_ids=true | all-gather | bytes 327680 | tf_op jit(solution)/shard_map/all_gather | solution.py:62
  65.0 16.9 %while.16 = (s32[]{:T(128)}, f32[4,4,2,512]{3,1,2,0:T(4,128)S(1)}, f32[4,2,2,4096]{3,1,0,2:T(2,128)S(1)}, f32[4,2,2,4096]{3,2,1,0:T(2,128)S(1)}, bf16[8192,512]{...) while((s32[]{:T(128)}, f32[4,4,2,512]{3,1,2,0:T(4,128)S(1)}, ...), condition=%wide.region_1.2_spmd.clone, body=%wide.region_0.1_spmd.clone.sunk | while | flops 35946508 | bytes 3932428 | solution.py:73
  65.3 0.1 pad_maximum_fusion.3
  65.5 1.3 %constant_dynamic-slice_fusion.7 = (bf16[512,512]{1,0:T(8,128)(2,1)S(1)}, bf16[512,512]{1,0:T(8,128)(2,1)S(1)}) fusion(bf16[8192,512]{1,0:T(8,128)(2,1)} %get-tuple-element.266, s32[]{:T(128)S(6)} %select_n.74, s32[]{:T(128)S(6)} %select_n.75), kind=kLoop, calls=%fused_computation.13.clone.1 | loop fusion | bytes 2097160 | tf_op jit(solution)/shard_map/while/body/eval_jaxpr/dynamic_slice | solution.py:25
  66.8 0.3 convolution_add_fusion.2
  67.4 0.1 pad_maximum_fusion.3
  67.6 1.3 %constant_dynamic-slice_fusion.7 = (bf16[512,512]{1,0:T(8,128)(2,1)S(1)}, bf16[512,512]{1,0:T(8,128)(2,1)S(1)}) fusion(bf16[8192,512]{1,0:T(8,128)(2,1)} %get-tuple-element.266, s32[]{:T(128)S(6)} %select_n.74, s32[]{:T(128)S(6)} %select_n.75), kind=kLoop, calls=%fused_computation.13.clone.1 | loop fusion | bytes 2097160 | tf_op jit(solution)/shard_map/while/body/eval_jaxpr/dynamic_slice | solution.py:25
  68.9 0.3 convolution_add_fusion.2
  69.5 0.1 pad_maximum_fusion.3
  69.7 1.3 %constant_dynamic-slice_fusion.7 = (bf16[512,512]{1,0:T(8,128)(2,1)S(1)}, bf16[512,512]{1,0:T(8,128)(2,1)S(1)}) fusion(bf16[8192,512]{1,0:T(8,128)(2,1)} %get-tuple-element.266, s32[]{:T(128)S(6)} %select_n.74, s32[]{:T(128)S(6)} %select_n.75), kind=kLoop, calls=%fused_computation.13.clone.1 | loop fusion | bytes 2097160 | tf_op jit(solution)/shard_map/while/body/eval_jaxpr/dynamic_slice | solution.py:25
  71.0 0.3 convolution_add_fusion.2
  71.6 0.1 pad_maximum_fusion.3
  71.9 1.3 %constant_dynamic-slice_fusion.7 = (bf16[512,512]{1,0:T(8,128)(2,1)S(1)}, bf16[512,512]{1,0:T(8,128)(2,1)S(1)}) fusion(bf16[8192,512]{1,0:T(8,128)(2,1)} %get-tuple-element.266, s32[]{:T(128)S(6)} %select_n.74, s32[]{:T(128)S(6)} %select_n.75), kind=kLoop, calls=%fused_computation.13.clone.1 | loop fusion | bytes 2097160 | tf_op jit(solution)/shard_map/while/body/eval_jaxpr/dynamic_slice | solution.py:25
  73.1 0.3 convolution_add_fusion.2
  73.8 0.1 pad_maximum_fusion.3
  74.0 1.3 %constant_dynamic-slice_fusion.7 = (bf16[512,512]{1,0:T(8,128)(2,1)S(1)}, bf16[512,512]{1,0:T(8,128)(2,1)S(1)}) fusion(bf16[8192,512]{1,0:T(8,128)(2,1)} %get-tuple-element.266, s32[]{:T(128)S(6)} %select_n.74, s32[]{:T(128)S(6)} %select_n.75), kind=kLoop, calls=%fused_computation.13.clone.1 | loop fusion | bytes 2097160 | tf_op jit(solution)/shard_map/while/body/eval_jaxpr/dynamic_slice | solution.py:25
  75.3 0.3 convolution_add_fusion.2
  75.9 0.1 pad_maximum_fusion.3
  76.1 1.3 %constant_dynamic-slice_fusion.7 = (bf16[512,512]{1,0:T(8,128)(2,1)S(1)}, bf16[512,512]{1,0:T(8,128)(2,1)S(1)}) fusion(bf16[8192,512]{1,0:T(8,128)(2,1)} %get-tuple-element.266, s32[]{:T(128)S(6)} %select_n.74, s32[]{:T(128)S(6)} %select_n.75), kind=kLoop, calls=%fused_computation.13.clone.1 | loop fusion | bytes 2097160 | tf_op jit(solution)/shard_map/while/body/eval_jaxpr/dynamic_slice | solution.py:25
  77.4 0.3 convolution_add_fusion.2
  78.0 0.1 pad_maximum_fusion.3
  78.2 1.3 %constant_dynamic-slice_fusion.7 = (bf16[512,512]{1,0:T(8,128)(2,1)S(1)}, bf16[512,512]{1,0:T(8,128)(2,1)S(1)}) fusion(bf16[8192,512]{1,0:T(8,128)(2,1)} %get-tuple-element.266, s32[]{:T(128)S(6)} %select_n.74, s32[]{:T(128)S(6)} %select_n.75), kind=kLoop, calls=%fused_computation.13.clone.1 | loop fusion | bytes 2097160 | tf_op jit(solution)/shard_map/while/body/eval_jaxpr/dynamic_slice | solution.py:25
  79.5 0.3 convolution_add_fusion.2
  80.1 0.1 pad_maximum_fusion.3
  80.3 1.3 %constant_dynamic-slice_fusion.7 = (bf16[512,512]{1,0:T(8,128)(2,1)S(1)}, bf16[512,512]{1,0:T(8,128)(2,1)S(1)}) fusion(bf16[8192,512]{1,0:T(8,128)(2,1)} %get-tuple-element.266, s32[]{:T(128)S(6)} %select_n.74, s32[]{:T(128)S(6)} %select_n.75), kind=kLoop, calls=%fused_computation.13.clone.1 | loop fusion | bytes 2097160 | tf_op jit(solution)/shard_map/while/body/eval_jaxpr/dynamic_slice | solution.py:25
  81.6 0.3 convolution_add_fusion.2
  82.0 11.5 %all-gather.1 = f32[4,1,2]{2,1,0:T(1,128)S(1)} all-gather(f32[1,1,2]{2,1,0:T(1,128)S(1)} %convert_bitcast_fusion), channel_id=1, replica_groups=mesh['grp'=2,'row'=4,'col'=4] {'row'}, dimensions={0}, use_global_device_ids=true | all-gather | bytes 40 | tf_op jit(solution)/shard_map/all_gather | solution.py:63
  93.7 5.0 %all-gather = f32[4,1,2]{2,1,0:T(1,128)S(1)} all-gather(f32[1,1,2]{2,1,0:T(1,128)S(1)} %convert_bitcast_fusion.1), channel_id=1, replica_groups=mesh['grp'=2,'row'=4,'col'=4] {'col'}, dimensions={0}, use_global_device_ids=true | all-gather | bytes 40 | tf_op jit(solution)/shard_map/all_gather | solution.py:55
  99.0 0.7 divide_multiply_fusion
  (63 shorter events, 3.0 us)
Async XLA Ops:
  36.3 7.3 %copy-start.1 = (f32[1,2,2,4096]{3,2,1,0:T(2,128)S(1)}, f32[1,2,2,4096]{3,2,1,0:T(2,128)}, u32[]{:S(2)}) copy-start(f32[1,2,2,4096]{3,2,1,0:T(2,128)} %param.7) | copy-start | bytes 196612
  36.3 14.6 %copy-start = (f32[1,2,2,4096]{3,2,1,0:T(2,128)S(1)}, f32[1,2,2,4096]{3,2,1,0:T(2,128)}, u32[]{:S(2)}) copy-start(f32[1,2,2,4096]{3,2,1,0:T(2,128)} %param.8) | copy-start | bytes 196612
  65.0 17.1 %copy-start.3 = (s32[1,2]{1,0:T(1,128)S(1)}, s32[1,2]{1,0:T(1,128)}, u32[]{:S(2)}) copy-start(s32[1,2]{1,0:T(1,128)} %param.10) | copy-start | bytes 28
  65.0 28.7 %copy-start.4 = (s32[1,2]{1,0:T(1,128)S(1)}, s32[1,2]{1,0:T(1,128)}, u32[]{:S(2)}) copy-start(s32[1,2]{1,0:T(1,128)} %param.9) | copy-start | bytes 28
  65.0 34.0 %copy-start.2 = (s32[4,4]{1,0:T(4,128)S(1)}, s32[4,4]{1,0:T(4,128)}, u32[]{:S(2)}) copy-start(s32[4,4]{1,0:T(4,128)} %param.11) | copy-start | bytes 196
where the time goes:
time: 100 us; the launch traced here: 99.7 us
  other arithmetic  46.8 us (47%)
  blocking collectives  37.9 us (38%)
  local copies, waits for them, and re-layouts  11.8 us (12%)
  matrix products  2.23 us (2%)
    another operation x9, other arithmetic  37.4 us
    all_gather x1, blocking collectives, body(): col_spec = lax.all_gather(n_spectra, 'row', axis=0, tiled=True)  14.1 us
    all_gather x1, blocking collectives, body(): piece_marks = lax.all_gather(n_marks, 'row', axis=0, tiled=True)  11.5 us
    dynamic_slice x8, local copies, waits for them, and re-layouts, band_rows(): real_rows = lax.dynamic_slice_in_dim(full_table, first_bin, band_width, 0)  10.2 us
    concatenate x1, other arithmetic, lag_table(): jnp.concatenate([weight * jnp.cos(angles), -weight * jnp.sin(angles)], 0)  7.26 us
    all_gather x1, blocking collectives, body(): lax.all_gather(z_spectra, 'col', axis=0, tiled=True)  7.23 us
    all_gather x1, blocking collectives, body(): lax.all_gather(z_flags.astype(jnp.float32), 'col', axis=0, tiled=True)  5.05 us
    dot_general x8, matrix products, correlate(): product = jnp.dot(merged, lag_tab, preferred_element_type=jnp.float32)  2.23 us

commit v1 on v0

v1 whole, which is shorter than its diff:
```python
import functools
import math

import jax
import jax.numpy as jnp
import numpy as np
from jax import lax
from jax.experimental import pallas as pl
from jax.experimental.pallas import tpu as pltpu
from jax.sharding import PartitionSpec as P

LAGS = 512
LANES = 128
DEPTH = 2 * LANES


def load_parts(ref, window, groups):
    base = window * 4 * groups
    return [ref[pl.ds(base + k, groups, stride=4), :] for k in (0, 2, 1, 3)]


def spread(ref, i, j, count):
    return jnp.broadcast_to(ref[i : i + 1, j : j + 1].astype(jnp.float32), (count, LANES))


def prepare_kernel(groups, lags, coarse_ref, fine_ref, inner_ref):
    steps = fine_ref.shape[0]
    fine_cos, fine_sin = fine_ref[:, :lags], fine_ref[:, lags:]
    for k in range(coarse_ref.shape[0]):
        coarse_cos, coarse_sin = coarse_ref[k : k + 1, :lags], coarse_ref[k : k + 1, lags:]
        cos = (coarse_cos * fine_cos - coarse_sin * fine_sin).astype(jnp.bfloat16)
        sin = (coarse_sin * fine_cos + coarse_cos * fine_sin).astype(jnp.bfloat16)
        top, low = pl.ds(k * steps, steps), pl.ds(DEPTH + k * steps, steps)
        inner_ref[top, :lags] = cos
        inner_ref[top, lags:] = sin
        inner_ref[low, :lags] = (0.0 - sin.astype(jnp.float32)).astype(jnp.bfloat16)
        inner_ref[low, lags:] = cos


def correlate_kernel(axes, z_count, n_count, windows, groups, lags, *refs):
    z_refs, refs = refs[:z_count], refs[z_count:]
    n_refs, refs = refs[:n_count], refs[n_count:]
    zf_refs, refs = refs[:z_count], refs[z_count:]
    nf_refs, refs = refs[:n_count], refs[n_count:]
    inner_ref, outer_ref, mask_ref, out_ref, lhs_ref, rows_ref = refs
    row = lax.broadcasted_iota(jnp.int32, (groups, LANES), 0)
    lane = lax.broadcasted_iota(jnp.int32, (groups, LANES), 1)
    first = jnp.where((row == 0) & (lane == 0), 0.5, 1.0)
    pairs = z_count * n_count
    for w in range(windows):
        for a in range(z_count):
            zr0, zr1, zi0, zi1 = load_parts(z_refs[a], w, groups)
            zr0, zi0 = zr0 * first, zi0 * first
            for b in range(n_count):
                nr0, nr1, ni0, ni1 = load_parts(n_refs[b], w, groups)
                at = pl.ds((w * pairs + a * n_count + b) * groups, groups)
                for k, part in enumerate(
                    (
                        zr0 * nr0 + zi0 * ni0,
                        zr1 * nr1 + zi1 * ni1,
                        zi0 * nr0 - zr0 * ni0,
                        zi1 * nr1 - zr1 * ni1,
                    )
                ):
                    lhs_ref[at, k * LANES : (k + 1) * LANES] = part.astype(jnp.bfloat16)
    product = jnp.dot(lhs_ref[...], inner_ref[...], preferred_element_type=jnp.float32)
    turned = product.reshape(windows * pairs, groups, 2 * lags) * outer_ref[...][None]
    turned = jnp.sum(turned, 1)
    corr = turned[:, :lags] + turned[:, lags:]
    unit = corr / jnp.sqrt(jnp.mean(corr * corr, 1, keepdims=True) + 1e-05)

    z_marks = jnp.concatenate(
        [spread(zf_refs[a], 0, w, n_count) for w in range(windows) for a in range(z_count)]
    )
    n_marks = jnp.concatenate(
        [
            spread(nf_refs[b], 0, w, 1)
            for w in range(windows)
            for a in range(z_count)
            for b in range(n_count)
        ]
    )
    unit = unit * (z_marks * n_marks)[:, :1]
    stacked, count = unit[:pairs], (z_marks * n_marks)[:pairs]
    for w in range(1, windows):
        stacked = stacked + unit[w * pairs : (w + 1) * pairs]
        count = count + (z_marks * n_marks)[w * pairs : (w + 1) * pairs]
    stacked = stacked / jnp.maximum(count, 1.0)[:, :1]
    z_at = place(axes[0], z_count)
    n_at = place(axes[1], n_count)
    for a in range(z_count):
        for b in range(n_count):
            k = a * n_count + b
            rows_ref[pl.ds(z_at(a) * n_count + n_at(b), 1), :] = stacked[k : k + 1]
    mask = jnp.concatenate(
        [spread(mask_ref, a, b, 1) for a in range(z_count) for b in range(n_count)]
    )
    rows_ref[...] = rows_ref[...] * mask[:, :1]
    for a in range(z_count):
        out_ref[a] = rows_ref[a * n_count : (a + 1) * n_count]


WHOLE = pl.BlockSpec(memory_space=pltpu.VMEM)


def prepare(bins, lags, fine=16):
    t = np.arange(lags) - lags // 2

    def turns(s):
        angle = np.pi / bins * ((s[:, None] * t[None, :]) % (2 * bins))
        return jnp.asarray(np.concatenate([np.cos(angle), np.sin(angle)], 1), jnp.float32)

    return pl.pallas_call(
        functools.partial(prepare_kernel, bins // DEPTH, lags),
        out_shape=jax.ShapeDtypeStruct((2 * DEPTH, 2 * lags), jnp.bfloat16),
        in_specs=[WHOLE] * 2,
        out_specs=WHOLE,
        compiler_params=pltpu.CompilerParams(vmem_limit_bytes=4 << 20),
        cost_estimate=pl.CostEstimate(flops=8 << 20, bytes_accessed=1 << 20, transcendentals=0),
    )(turns(np.arange(0, DEPTH, fine)), turns(np.arange(fine)))


def outer_table(bins, lags):
    t = np.arange(lags) - lags // 2
    angle = np.pi / bins * ((DEPTH * np.arange(bins // DEPTH)[:, None] * t[None, :]) % (2 * bins))
    return jnp.asarray(2.0 * np.concatenate([np.cos(angle), -np.sin(angle)], 1), jnp.float32)


def correlate(axes, z_blocks, z_flags, n_blocks, n_flags, mask, inner, bins):
    z_count, n_count = len(z_blocks), len(n_blocks)
    windows = z_flags[0].shape[1]
    groups, pairs = bins // DEPTH, z_count * n_count
    return pl.pallas_call(
        functools.partial(correlate_kernel, axes, z_count, n_count, windows, groups, LAGS),
        out_shape=jax.ShapeDtypeStruct((z_count, n_count, LAGS), jnp.float32),
        in_specs=[WHOLE] * (2 * z_count + 2 * n_count + 3),
        out_specs=WHOLE,
        scratch_shapes=[
            pltpu.VMEM((windows * pairs * groups, 2 * DEPTH), jnp.bfloat16),
            pltpu.VMEM((pairs, LAGS), jnp.float32),
        ],
        compiler_params=pltpu.CompilerParams(vmem_limit_bytes=16 << 20),
        cost_estimate=pl.CostEstimate(flops=512 << 20, bytes_accessed=1 << 20, transcendentals=0),
    )(*z_blocks, *n_blocks, *z_flags, *n_flags, inner, outer_table(bins, LAGS), mask)


def as_rows(block):
    _, windows, parts, bins = block.shape
    block = block.reshape(windows, parts, bins // LANES, LANES)
    return jnp.swapaxes(block, 1, 2).reshape(windows * parts * bins // LANES, LANES)


def partners(size):
    if size & (size - 1) == 0:
        return [[(i, i ^ k) for i in range(size)] for k in range(1, size)]
    return [[(i, (i + k) % size) for i in range(size)] for k in range(1, size)]


def gather(block, axis, size):
    return [block] + [lax.ppermute(block, axis, to) for to in partners(size)]


def place(axis, size):
    if axis is None:
        return lambda k: k
    me = lax.axis_index(axis)
    if size & (size - 1) == 0:
        return lambda k: me ^ k
    return lambda k: lax.rem(me + size - k, size)


SMALL = 8


def body(sizes, z_spectra, n_spectra, z_flags, n_flags, pair_mask):
    bins = z_spectra.shape[-1]
    rows, cols = sizes
    z_own, n_own = as_rows(z_spectra), as_rows(n_spectra)
    inner = prepare(bins, LAGS)
    z_blocks, z_marks = gather(z_own, "col", cols), gather(z_flags, "col", cols)
    if rows <= SMALL:
        n_blocks, n_marks = gather(n_own, "row", rows), gather(n_flags, "row", rows)
        return correlate(
            ("col", "row"), z_blocks, z_marks, n_blocks, n_marks, pair_mask, inner, bins
        )
    n_all = lax.all_gather(n_own, "row", axis=0)
    n_marks = lax.all_gather(n_flags.astype(jnp.float32), "row", axis=0)
    step = math.gcd(rows, 4)
    count = rows // step

    def one(args):
        blocks, marks, mask = args
        return correlate(
            ("col", None), z_blocks, z_marks, list(blocks), list(marks), mask, inner, bins
        )

    stacks = lax.map(
        one,
        (
            n_all.reshape((count, step) + n_own.shape),
            n_marks.reshape((count, step) + n_flags.shape),
            jnp.moveaxis(pair_mask.reshape(-1, count, step), 1, 0),
        ),
    )
    return jnp.moveaxis(stacks, 0, 1).reshape(len(z_blocks), rows, LAGS)


def solution(mesh):
    placed = (
        P(("grp", "row", "col"), None, None, None),
        P(("grp", "col", "row"), None, None, None),
        P(("grp", "row", "col"), None),
        P(("grp", "col", "row"), None),
        P(("grp", "row"), "col"),
    )
    sizes = (mesh.shape["row"], mesh.shape["col"])
    return jax.shard_map(
        functools.partial(body, sizes),
        mesh=mesh,
        in_specs=placed,
        out_specs=P(("grp", "row"), "col", None),
        check_vma=False,
    )
```

time: 100 us -> 22.8 us (0.23)
  other arithmetic: 46.8 us -> 0 us
  blocking collectives: 37.9 us -> 0 us
  starting transfers between devices: 0 us -> 15.8 us
  local copies, waits for them, and re-layouts: 11.8 us -> 1.7 us
  waiting for transfers between devices: 0 us -> 3.23 us
  matrix products: 2.23 us -> 0 us
  Pallas kernels: 0 us -> 1.75 us
    another operation x17 -> x0, other arithmetic: 38.6 us -> none
    all_gather x4 -> x0, blocking collectives: 37.9 us -> none  [the longest x1 14.1 us: body(): col_spec = lax.all_gather(n_spectra, 'row', axis=0, tiled=True)]
    ppermute x0 -> x12, starting transfers between devices: none -> 15.8 us  [gather(): return [block] + [lax.ppermute(block, axis, to) for to in partners(size)]]
    dynamic_slice x8 -> x0, local copies, waits for them, and re-layouts: 10.2 us -> none  [band_rows(): real_rows = lax.dynamic_slice_in_dim(full_table, first_bin, band_width, 0)]
    concatenate x1 -> x0, other arithmetic: 7.26 us -> none  [lag_table(): jnp.concatenate([weight * jnp.cos(angles), -weight * jnp.sin(angles)], 0)]
    ppermute x0 -> x12, waiting for transfers between devices: none -> 3.23 us  [gather(): return [block] + [lax.ppermute(block, axis, to) for to in partners(size)]]
    dot_general x8 -> x0, matrix products: 2.23 us -> none  [correlate(): product = jnp.dot(merged, lag_tab, preferred_element_type=jnp.float32)]
    pallas_call x0 -> x2, Pallas kernels: none -> 1.75 us  [the longest x1 1.56 us: correlate(): pl.pallas_call(functools.partial(correlate_kernel, axes, z_count, n_count...]
  transfers between devices with their start and end apart: 0 -> 12, of which waited for: 0 -> 3; matrix products, arithmetic and copies ran while one was open for 0% -> 0% of each run, Pallas kernels for 0% -> 1%
where the time goes in v1:
time: 22.8 us; the launch traced here: 22.6 us
  starting transfers between devices  15.8 us (69%)
  waiting for transfers between devices  3.23 us (14%)
  Pallas kernels  1.75 us (8%)
  local copies, waits for them, and re-layouts  1.7 us (7%)
    ppermute x12, starting transfers between devices, gather(): return [block] + [lax.ppermute(block, axis, to) for to in partners(size)]  15.8 us
    ppermute x12, waiting for transfers between devices, gather(): return [block] + [lax.ppermute(block, axis, to) for to in partners(size)]  3.23 us
    unnamed x16, local copies, waits for them, and re-layouts  1.7 us
    pallas_call x1, Pallas kernels, correlate(): pl.pallas_call(functools.partial(correlate_kernel, axes, z_count, n_count...  1.56 us
  transfers between devices with their start and end apart: 12, of which 3 were waited for; matrix products, arithmetic and copies ran while one was open for 0% of the time, Pallas kernels for 1%

profile of v1, /device:TPU:0, one launch (start us, length us, event | category | flops | bytes accessed | tf_op | source)
XLA Modules:
  0.0 22.6 jit_solution(15105835885663493630)
XLA Ops:
  0.0 2.4 %collective-permute-start.2 = (f32[128,128]{1,0:T(8,128)}, f32[128,128]{1,0:T(8,128)S(1)}, u32[]{:S(2)}, u32[]{:S(2)}) collective-permute-start(f32[128,128]{1,0:T(8,128)} %bitcast.10), channel_id=1, source_target_pairs={{0,3},{1,2},{2,1},{3,0},{4,7},{5,6},{6,5},{7,4},{8,11},{9,10},{10,... | collective-permute-start | bytes 196616 | tf_op jit(solution)/shard_map/ppermute | solution.py:160
  2.4 0.0 copy-done.5
  2.4 1.2 %collective-permute-start.7 = (s32[1,2]{1,0:T(1,128)S(1)}, s32[1,2]{1,0:T(1,128)S(1)}, u32[]{:S(2)}, u32[]{:S(2)}) collective-permute-start(s32[1,2]{1,0:T(1,128)S(1)} %copy-done.5), channel_id=1, source_target_pairs={{0,2},{1,3},{2,0},{3,1},{4,6},{5,7},{6,4},{7,5},{8,10},{9,11},{10,... | collective-permute-start | bytes 32 | tf_op jit(solution)/shard_map/ppermute | solution.py:160
  3.6 0.0 collective-permute-start.6
  3.6 0.9 %collective-permute-start.8 = (s32[1,2]{1,0:T(1,128)S(1)}, s32[1,2]{1,0:T(1,128)S(1)}, u32[]{:S(2)}, u32[]{:S(2)}) collective-permute-start(s32[1,2]{1,0:T(1,128)S(1)} %copy-done.5), channel_id=1, source_target_pairs={{0,3},{1,2},{2,1},{3,0},{4,7},{5,6},{6,5},{7,4},{8,11},{9,10},{10,... | collective-permute-start | bytes 32 | tf_op jit(solution)/shard_map/ppermute | solution.py:160
  4.6 0.0 copy-done.6
  4.6 2.6 %collective-permute-start.10 = (s32[1,2]{1,0:T(1,128)S(1)}, s32[1,2]{1,0:T(1,128)S(1)}, u32[]{:S(2)}, u32[]{:S(2)}) collective-permute-start(s32[1,2]{1,0:T(1,128)S(1)} %copy-done.6), channel_id=1, source_target_pairs={{0,8},{4,12},{8,0},{12,4},{1,9},{5,13},{9,1},{13,5},{2,10},{6,14},... | collective-permute-start | bytes 32 | tf_op jit(solution)/shard_map/ppermute | solution.py:160
  7.1 0.0 collective-permute-done.7.refs_10_
  7.2 1.6 %collective-permute-start.9 = (s32[1,2]{1,0:T(1,128)S(1)}, s32[1,2]{1,0:T(1,128)S(1)}, u32[]{:S(2)}, u32[]{:S(2)}) collective-permute-start(s32[1,2]{1,0:T(1,128)S(1)} %copy-done.6), channel_id=1, source_target_pairs={{0,4},{4,0},{8,12},{12,8},{1,5},{5,1},{9,13},{13,9},{2,6},{6,2},{1... | collective-permute-start | bytes 32 | tf_op jit(solution)/shard_map/ppermute | solution.py:160
  8.7 0.0 collective-permute-done.6.refs_9_
  8.7 1.4 %collective-permute-start.11 = (s32[1,2]{1,0:T(1,128)S(1)}, s32[1,2]{1,0:T(1,128)S(1)}, u32[]{:S(2)}, u32[]{:S(2)}) collective-permute-start(s32[1,2]{1,0:T(1,128)S(1)} %copy-done.6), channel_id=1, source_target_pairs={{0,12},{4,8},{8,4},{12,0},{1,13},{5,9},{9,5},{13,1},{2,14},{6,10},... | collective-permute-start | bytes 32 | tf_op jit(solution)/shard_map/ppermute | solution.py:160
  10.2 0.0 collective-permute-done.8.refs_11_
  10.2 1.5 %collective-permute-start.1 = (f32[128,128]{1,0:T(8,128)}, f32[128,128]{1,0:T(8,128)S(1)}, u32[]{:S(2)}, u32[]{:S(2)}) collective-permute-start(f32[128,128]{1,0:T(8,128)} %bitcast.11), channel_id=1, source_target_pairs={{0,2},{1,3},{2,0},{3,1},{4,6},{5,7},{6,4},{7,5},{8,10},{9,11},{10,... | collective-permute-start | bytes 196616 | tf_op jit(solution)/shard_map/ppermute | solution.py:160
  11.6 0.0 collective-permute-done.10.refs_14_
  11.7 0.0 collective-permute-start
  11.7 0.0 collective-permute-done.9.refs_13_
  11.7 2.2 %collective-permute-start.5 = (f32[128,128]{1,0:T(8,128)}, f32[128,128]{1,0:T(8,128)S(1)}, u32[]{:S(2)}, u32[]{:S(2)}) collective-permute-start(f32[128,128]{1,0:T(8,128)} %bitcast.14), channel_id=1, source_target_pairs={{0,12},{4,8},{8,4},{12,0},{1,13},{5,9},{9,5},{13,1},{2,14},{6,10},... | collective-permute-start | bytes 196616 | tf_op jit(solution)/shard_map/ppermute | solution.py:160
  13.8 0.3 %collective-permute-done.11.refs_15_ = s32[1,2]{1,0:T(1,128)S(1)} collective-permute-done((s32[1,2]{1,0:T(1,128)S(1)}, s32[1,2]{1,0:T(1,128)S(1)}, u32[]{:S(2)}, u32[]{:S(2)}) %collective-permute-start.11) | collective-permute-done | bytes 40 | tf_op jit(solution)/shard_map/ppermute | solution.py:160
  14.1 0.0 collective-permute-start.4
  14.1 0.0 collective-permute-done.2.refs_3_
  14.1 2.0 %collective-permute-start.3 = (f32[128,128]{1,0:T(8,128)}, f32[128,128]{1,0:T(8,128)S(1)}, u32[]{:S(2)}, u32[]{:S(2)}) collective-permute-start(f32[128,128]{1,0:T(8,128)} %bitcast.16), channel_id=1, source_target_pairs={{0,4},{4,0},{8,12},{12,8},{1,5},{5,1},{9,13},{13,9},{2,6},{6,2},{1... | collective-permute-start | bytes 196616 | tf_op jit(solution)/shard_map/ppermute | solution.py:160
  16.1 0.8 %copy-done = f32[16,1024]{1,0:T(8,128)S(1)} copy-done((f32[16,1024]{1,0:T(8,128)S(1)}, f32[16,1024]{1,0:T(8,128)}, u32[]{:S(2)}) %copy-start) | copy-done | bytes 65560
  17.0 0.8 %copy-done.1 = f32[16,1024]{1,0:T(8,128)S(1)} copy-done((f32[16,1024]{1,0:T(8,128)S(1)}, f32[16,1024]{1,0:T(8,128)}, u32[]{:S(2)}) %copy-start.1) | copy-done | bytes 65560
  17.8 0.2 shard_map.82.refs_16_
  18.0 0.0 collective-permute-done.1.refs_2_
  18.0 0.0 collective-permute-done.refs_1_
  18.0 0.8 %collective-permute-done.5.refs_7_ = f32[128,128]{1,0:T(8,128)S(1)} collective-permute-done((f32[128,128]{1,0:T(8,128)}, f32[128,128]{1,0:T(8,128)S(1)}, u32[]{:S(2)}, u32[]{:S(2)}) %collective-permute-start.5) | collective-permute-done | bytes 65568 | tf_op jit(solution)/shard_map/ppermute | solution.py:160
  18.8 2.2 %collective-permute-done.4.refs_6_ = f32[128,128]{1,0:T(8,128)S(1)} collective-permute-done((f32[128,128]{1,0:T(8,128)}, f32[128,128]{1,0:T(8,128)S(1)}, u32[]{:S(2)}, u32[]{:S(2)}) %collective-permute-start.4) | collective-permute-done | bytes 65568 | tf_op jit(solution)/shard_map/ppermute | solution.py:160
  21.0 0.0 collective-permute-done.3.refs_5_
  21.0 0.0 copy-done.3
  21.0 0.0 copy-done.4
  21.0 1.6 %shard_map.83 = f32[4,4,512]{2,1,0:T(4,128)} custom-call(f32[128,128]{1,0:T(8,128)S(1)} %bitcast.13, f32[128,128]{1,0:T(8,128)S(1)} %collective-permute-done.refs_1_, f32[128,128]{1,0:T(8,128)S(1)} %collective-permute-done.1.refs_2_, f32[128,128]{1,0:T(8,128)S(1)} %collective-permute-done.2.refs_3_, f32[128,128]{1,0:T(8,128)S(1)} %bitcast.17, ...), custom_call_target="tpu_custom_call" | custom-call | flops 536870912 | bytes 1048576 | tf_op jit(solution)/shard_map/pallas_call | solution.py:133
  (10 shorter events, 0.0 us)
Async XLA Ops:
  0.0 2.4 %copy-start.5 = (s32[1,2]{1,0:T(1,128)S(1)}, s32[1,2]{1,0:T(1,128)}, u32[]{:S(2)}) copy-start(s32[1,2]{1,0:T(1,128)} %refs_8_.1) | copy-start | bytes 28
  0.0 4.6 %copy-start.6 = (s32[1,2]{1,0:T(1,128)S(1)}, s32[1,2]{1,0:T(1,128)}, u32[]{:S(2)}) copy-start(s32[1,2]{1,0:T(1,128)} %refs_12_.1) | copy-start | bytes 28
  0.0 14.1 %collective-permute-start.2 = (f32[128,128]{1,0:T(8,128)}, f32[128,128]{1,0:T(8,128)S(1)}, u32[]{:S(2)}, u32[]{:S(2)}) collective-permute-start(f32[128,128]{1,0:T(8,128)} %bitcast.10), channel_id=1, source_target_pairs={{0,3},{1,2},{2,1},{3,0},{4,7},{5,6},{6,5},{7,4},{8,11},{9,10},{10,... | collective-permute-start | bytes 196616 | tf_op jit(solution)/shard_map/ppermute | solution.py:160
  2.4 4.7 %collective-permute-start.7 = (s32[1,2]{1,0:T(1,128)S(1)}, s32[1,2]{1,0:T(1,128)S(1)}, u32[]{:S(2)}, u32[]{:S(2)}) collective-permute-start(s32[1,2]{1,0:T(1,128)S(1)} %copy-done.5), channel_id=1, source_target_pairs={{0,2},{1,3},{2,0},{3,1},{4,6},{5,7},{6,4},{7,5},{8,10},{9,11},{10,... | collective-permute-start | bytes 32 | tf_op jit(solution)/shard_map/ppermute | solution.py:160
  3.6 5.1 %collective-permute-start.6 = (s32[1,2]{1,0:T(1,128)S(1)}, s32[1,2]{1,0:T(1,128)S(1)}, u32[]{:S(2)}, u32[]{:S(2)}) collective-permute-start(s32[1,2]{1,0:T(1,128)S(1)} %copy-done.5), channel_id=1, source_target_pairs={{0,1},{1,0},{2,3},{3,2},{4,5},{5,4},{6,7},{7,6},{8,9},{9,8},{10,11... | collective-permute-start | bytes 32 | tf_op jit(solution)/shard_map/ppermute | solution.py:160
  3.6 6.5 %collective-permute-start.8 = (s32[1,2]{1,0:T(1,128)S(1)}, s32[1,2]{1,0:T(1,128)S(1)}, u32[]{:S(2)}, u32[]{:S(2)}) collective-permute-start(s32[1,2]{1,0:T(1,128)S(1)} %copy-done.5), channel_id=1, source_target_pairs={{0,3},{1,2},{2,1},{3,0},{4,7},{5,6},{6,5},{7,4},{8,11},{9,10},{10,... | collective-permute-start | bytes 32 | tf_op jit(solution)/shard_map/ppermute | solution.py:160
  4.6 7.1 %collective-permute-start.10 = (s32[1,2]{1,0:T(1,128)S(1)}, s32[1,2]{1,0:T(1,128)S(1)}, u32[]{:S(2)}, u32[]{:S(2)}) collective-permute-start(s32[1,2]{1,0:T(1,128)S(1)} %copy-done.6), channel_id=1, source_target_pairs={{0,8},{4,12},{8,0},{12,4},{1,9},{5,13},{9,1},{13,5},{2,10},{6,14},... | collective-permute-start | bytes 32 | tf_op jit(solution)/shard_map/ppermute | solution.py:160
  7.2 4.5 %collective-permute-start.9 = (s32[1,2]{1,0:T(1,128)S(1)}, s32[1,2]{1,0:T(1,128)S(1)}, u32[]{:S(2)}, u32[]{:S(2)}) collective-permute-start(s32[1,2]{1,0:T(1,128)S(1)} %copy-done.6), channel_id=1, source_target_pairs={{0,4},{4,0},{8,12},{12,8},{1,5},{5,1},{9,13},{13,9},{2,6},{6,2},{1... | collective-permute-start | bytes 32 | tf_op jit(solution)/shard_map/ppermute | solution.py:160
  8.7 5.4 %collective-permute-start.11 = (s32[1,2]{1,0:T(1,128)S(1)}, s32[1,2]{1,0:T(1,128)S(1)}, u32[]{:S(2)}, u32[]{:S(2)}) collective-permute-start(s32[1,2]{1,0:T(1,128)S(1)} %copy-done.6), channel_id=1, source_target_pairs={{0,12},{4,8},{8,4},{12,0},{1,13},{5,9},{9,5},{13,1},{2,14},{6,10},... | collective-permute-start | bytes 32 | tf_op jit(solution)/shard_map/ppermute | solution.py:160
  10.2 7.9 %collective-permute-start.1 = (f32[128,128]{1,0:T(8,128)}, f32[128,128]{1,0:T(8,128)S(1)}, u32[]{:S(2)}, u32[]{:S(2)}) collective-permute-start(f32[128,128]{1,0:T(8,128)} %bitcast.11), channel_id=1, source_target_pairs={{0,2},{1,3},{2,0},{3,1},{4,6},{5,7},{6,4},{7,5},{8,10},{9,11},{10,... | collective-permute-start | bytes 196616 | tf_op jit(solution)/shard_map/ppermute | solution.py:160
  11.7 6.4 %collective-permute-start = (f32[128,128]{1,0:T(8,128)}, f32[128,128]{1,0:T(8,128)S(1)}, u32[]{:S(2)}, u32[]{:S(2)}) collective-permute-start(f32[128,128]{1,0:T(8,128)} %bitcast.12), channel_id=1, source_target_pairs={{0,1},{1,0},{2,3},{3,2},{4,5},{5,4},{6,7},{7,6},{8,9},{9,8},{10,11... | collective-permute-start | bytes 196616 | tf_op jit(solution)/shard_map/ppermute | solution.py:160
  11.7 7.1 %collective-permute-start.5 = (f32[128,128]{1,0:T(8,128)}, f32[128,128]{1,0:T(8,128)S(1)}, u32[]{:S(2)}, u32[]{:S(2)}) collective-permute-start(f32[128,128]{1,0:T(8,128)} %bitcast.14), channel_id=1, source_target_pairs={{0,12},{4,8},{8,4},{12,0},{1,13},{5,9},{9,5},{13,1},{2,14},{6,10},... | collective-permute-start | bytes 196616 | tf_op jit(solution)/shard_map/ppermute | solution.py:160
  14.1 6.9 %collective-permute-start.4 = (f32[128,128]{1,0:T(8,128)}, f32[128,128]{1,0:T(8,128)S(1)}, u32[]{:S(2)}, u32[]{:S(2)}) collective-permute-start(f32[128,128]{1,0:T(8,128)} %bitcast.15), channel_id=1, source_target_pairs={{0,8},{4,12},{8,0},{12,4},{1,9},{5,13},{9,1},{13,5},{2,10},{6,14},... | collective-permute-start | bytes 196616 | tf_op jit(solution)/shard_map/ppermute | solution.py:160
  14.1 6.9 %collective-permute-start.3 = (f32[128,128]{1,0:T(8,128)}, f32[128,128]{1,0:T(8,128)S(1)}, u32[]{:S(2)}, u32[]{:S(2)}) collective-permute-start(f32[128,128]{1,0:T(8,128)} %bitcast.16), channel_id=1, source_target_pairs={{0,4},{4,0},{8,12},{12,8},{1,5},{5,1},{9,13},{13,9},{2,6},{6,2},{1... | collective-permute-start | bytes 196616 | tf_op jit(solution)/shard_map/ppermute | solution.py:160
  16.1 0.8 %copy-start = (f32[16,1024]{1,0:T(8,128)S(1)}, f32[16,1024]{1,0:T(8,128)}, u32[]{:S(2)}) copy-start(f32[16,1024]{1,0:T(8,128)} %constant.7.clone.fine_ref) | copy-start | bytes 196612
  17.0 0.8 %copy-start.1 = (f32[16,1024]{1,0:T(8,128)S(1)}, f32[16,1024]{1,0:T(8,128)}, u32[]{:S(2)}) copy-start(f32[16,1024]{1,0:T(8,128)} %constant.6.clone.coarse_ref) | copy-start | bytes 196612
  17.8 3.2 %copy-start.2 = (f32[1,2,2,4096]{3,2,1,0:T(2,128)S(1)}, f32[1,2,2,4096]{3,2,1,0:T(2,128)}, u32[]{:S(2)}) copy-start(f32[1,2,2,4096]{3,2,1,0:T(2,128)} %param.8) | copy-start | bytes 196612
  17.8 3.2 %copy-start.3 = (f32[1,2,2,4096]{3,2,1,0:T(2,128)S(1)}, f32[1,2,2,4096]{3,2,1,0:T(2,128)}, u32[]{:S(2)}) copy-start(f32[1,2,2,4096]{3,2,1,0:T(2,128)} %param.9) | copy-start | bytes 196612
  17.8 3.2 %copy-start.4 = (s32[4,4]{1,0:T(4,128)S(1)}, s32[4,4]{1,0:T(4,128)}, u32[]{:S(2)}) copy-start(s32[4,4]{1,0:T(4,128)} %refs_18_.1) | copy-start | bytes 196
  17.8 3.2 %copy-start.7 = (f32[16,1024]{1,0:T(8,128)S(1)}, f32[16,1024]{1,0:T(8,128)}, u32[]{:S(2)}) copy-start(f32[16,1024]{1,0:T(8,128)} %constant.8.clone.refs_17_) | copy-start | bytes 196612

commit v2 on v1

v2 whole, which is shorter than its diff:
```python
import functools
import math

import jax
import jax.numpy as jnp
import numpy as np
from jax import lax
from jax.experimental import pallas as pl
from jax.experimental.pallas import tpu as pltpu
from jax.sharding import PartitionSpec as P


LAGS = 512
LANES = 128
SUBLANES = 8
DEPTH = 2 * LANES
WHOLE = pl.BlockSpec(memory_space=pltpu.VMEM)
OPENF = 1 << 30

STAGES = ((0, 0, 0, 1), (0, 0, 0, 0))


def spread(ref, i, j, count=1):
    return jnp.broadcast_to(ref[i : i + 1, j : j + 1].astype(jnp.float32), (count, LANES))


def open_kernel(out_ref):
    out_ref[...] = jnp.zeros(out_ref.shape, out_ref.dtype)


def opening():
    return pl.pallas_call(
        open_kernel,
        out_shape=jax.ShapeDtypeStruct((SUBLANES, LANES), jnp.float32),
        out_specs=WHOLE,
        compiler_params=pltpu.CompilerParams(vmem_limit_bytes=1 << 20),
        cost_estimate=pl.CostEstimate(flops=OPENF, bytes_accessed=1 << 12, transcendentals=0),
    )()


def pack_kernel(block_ref, flag_ref, blank_ref, out_ref):
    rows, windows = block_ref.shape[0], flag_ref.shape[1]
    out_ref[:rows] = block_ref[...]
    lane = lax.broadcasted_iota(jnp.int32, (SUBLANES, LANES), 1)
    flags = blank_ref[...]
    for w in range(windows):
        flags = jnp.where(lane == w, spread(flag_ref, 0, w, SUBLANES), flags)
    out_ref[rows:] = flags


def pack(block, flags, blank):
    rows = block.shape[0]
    return pl.pallas_call(
        pack_kernel,
        out_shape=jax.ShapeDtypeStruct((rows + SUBLANES, LANES), jnp.float32),
        in_specs=[WHOLE] * 3,
        out_specs=WHOLE,
        compiler_params=pltpu.CompilerParams(vmem_limit_bytes=2 << 20),
    )(block, flags, blank)


def prepare_kernel(lags, coarse_ref, fine_ref, inner_ref):
    steps = fine_ref.shape[0]
    fine_cos, fine_sin = fine_ref[:, :lags], fine_ref[:, lags:]
    for k in range(coarse_ref.shape[0]):
        coarse_cos, coarse_sin = coarse_ref[k : k + 1, :lags], coarse_ref[k : k + 1, lags:]
        cos = (coarse_cos * fine_cos - coarse_sin * fine_sin).astype(jnp.bfloat16)
        sin = (coarse_sin * fine_cos + coarse_cos * fine_sin).astype(jnp.bfloat16)
        top, low = pl.ds(k * steps, steps), pl.ds(DEPTH + k * steps, steps)
        inner_ref[top, :lags] = cos
        inner_ref[top, lags:] = sin
        inner_ref[low, :lags] = (0.0 - sin.astype(jnp.float32)).astype(jnp.bfloat16)
        inner_ref[low, lags:] = cos


def turns(bins, lags, s):
    t = np.arange(lags) - lags // 2
    angle = np.pi / bins * ((s[:, None] * t[None, :]) % (2 * bins))
    return np.cos(angle), np.sin(angle)


def prepare(bins, lags, fine=16):
    near = [
        jnp.asarray(np.concatenate(turns(bins, lags, s), 1), jnp.float32)
        for s in (np.arange(0, DEPTH, fine), np.arange(fine))
    ]
    return pl.pallas_call(
        functools.partial(prepare_kernel, lags),
        out_shape=jax.ShapeDtypeStruct((2 * DEPTH, 2 * lags), jnp.bfloat16),
        in_specs=[WHOLE] * 2,
        out_specs=WHOLE,
        compiler_params=pltpu.CompilerParams(vmem_limit_bytes=4 << 20),
        cost_estimate=pl.CostEstimate(flops=8 << 20, bytes_accessed=1 << 20, transcendentals=0),
    )(*near)


def outer_table(bins, lags):
    cos, sin = turns(bins, lags, np.arange(0, bins, DEPTH))
    return jnp.asarray(2.0 * np.concatenate([cos, -sin], 1), jnp.float32)


def load_parts(ref, window, groups):
    base = window * 4 * groups
    return [ref[pl.ds(base + k, groups, stride=4), :] for k in (0, 2, 1, 3)]


def stack_pairs(windows, groups, lags, z_refs, n_refs, pairs, inner_ref, outer_ref, lhs_ref):
    row = lax.broadcasted_iota(jnp.int32, (groups, LANES), 0)
    lane = lax.broadcasted_iota(jnp.int32, (groups, LANES), 1)
    first = jnp.where((row == 0) & (lane == 0), 0.5, 1.0)
    count = len(pairs)
    for w in range(windows):
        for p, (a, b) in enumerate(pairs):
            zr0, zr1, zi0, zi1 = load_parts(z_refs[a], w, groups)
            zr0, zi0 = zr0 * first, zi0 * first
            nr0, nr1, ni0, ni1 = load_parts(n_refs[b], w, groups)
            parts = (
                zr0 * nr0 + zi0 * ni0,
                zr1 * nr1 + zi1 * ni1,
                zi0 * nr0 - zr0 * ni0,
                zi1 * nr1 - zr1 * ni1,
            )
            at = pl.ds((w * count + p) * groups, groups)
            for k, part in enumerate(parts):
                lhs_ref[at, k * LANES : (k + 1) * LANES] = part.astype(jnp.bfloat16)
    product = jnp.dot(lhs_ref[...], inner_ref[...], preferred_element_type=jnp.float32)
    turned = product.reshape(windows * count, groups, 2 * lags) * outer_ref[...][None]
    turned = jnp.sum(turned, 1)
    corr = turned[:, :lags] + turned[:, lags:]
    unit = corr / jnp.sqrt(jnp.mean(corr * corr, 1, keepdims=True) + 1e-05)
    flag_row = 4 * windows * groups
    marks = [
        jnp.concatenate([spread(z_refs[a], flag_row, w) for a, _ in pairs])
        * jnp.concatenate([spread(n_refs[b], flag_row, w) for _, b in pairs])
        for w in range(windows)
    ]
    total = sum(unit[w * count : (w + 1) * count] * marks[w][:, :1] for w in range(windows))
    return total / jnp.maximum(sum(marks), 1.0)[:, :1]


def stage_kernel(shape, lags, z_count, n_count, pairs, *refs):
    z_refs, n_refs = refs[:z_count], refs[z_count : z_count + n_count]
    inner_ref, outer_ref, out_ref, lhs_ref = refs[z_count + n_count :]
    out_ref[...] = stack_pairs(*shape, lags, z_refs, n_refs, pairs, inner_ref, outer_ref, lhs_ref)


def last_kernel(shape, lags, z_count, n_count, pairs, earlier, axes, *refs):
    z_refs, n_refs = refs[:z_count], refs[z_count : z_count + n_count]
    refs = refs[z_count + n_count :]
    done_refs, (inner_ref, outer_ref, mask_ref, out_ref, lhs_ref, rows_ref) = refs[:-6], refs[-6:]
    z_all, n_all = mask_ref.shape
    z_at, n_at = place(axes[0], z_all), place(axes[1], n_all)

    def put(a, b, row):
        rows_ref[pl.ds(z_at(a) * n_all + n_at(b), 1), :] = row

    for ref, slots in zip(done_refs, earlier):
        for k, (a, b) in enumerate(slots):
            put(a, b, ref[k : k + 1])
    mask = [
        jnp.concatenate([spread(mask_ref, a, b) for b in range(n_all)]) for a in range(z_all)
    ]
    local = [(pairs[0].index(a), pairs[1].index(b)) for a, b in pairs[2]]
    stacked = stack_pairs(*shape, lags, z_refs, n_refs, local, inner_ref, outer_ref, lhs_ref)
    for k, (a, b) in enumerate(pairs[2]):
        put(a, b, stacked[k : k + 1])
    for a in range(z_all):
        out_ref[a] = rows_ref[a * n_all : (a + 1) * n_all] * mask[a][:, :1]


def correlate(axes, stages, z_blocks, n_blocks, mask, inner, windows, bins):
    shape = (windows, bins // DEPTH)
    z_stage, n_stage = stages
    last = max(z_stage + n_stage)
    outer = outer_table(bins, LAGS)
    done, earlier = [], []
    for stage in range(last + 1):
        slots = [
            (a, b)
            for a in range(len(z_blocks))
            for b in range(len(n_blocks))
            if max(z_stage[a], n_stage[b]) == stage
        ]
        if not slots:
            continue
        z_used, n_used = (sorted(set(s)) for s in zip(*slots))
        count = len(slots)
        lhs = pltpu.VMEM((windows * count * shape[1], 2 * DEPTH), jnp.bfloat16)
        arrays = [z_blocks[a] for a in z_used] + [n_blocks[b] for b in n_used]
        settings = dict(
            out_specs=WHOLE,
            compiler_params=pltpu.CompilerParams(vmem_limit_bytes=16 << 20),
            cost_estimate=pl.CostEstimate(
                flops=count << 25, bytes_accessed=count << 16, transcendentals=0
            ),
        )
        if stage < last:
            local = [(z_used.index(a), n_used.index(b)) for a, b in slots]
            done.append(
                pl.pallas_call(
                    functools.partial(stage_kernel, shape, LAGS, len(z_used), len(n_used), local),
                    out_shape=jax.ShapeDtypeStruct((count, LAGS), jnp.float32),
                    in_specs=[WHOLE] * (len(arrays) + 2),
                    scratch_shapes=[lhs],
                    **settings,
                )(*arrays, inner, outer)
            )
            earlier.append(slots)
            continue
        used = (z_used, n_used, slots)
        return pl.pallas_call(
            functools.partial(
                last_kernel, shape, LAGS, len(z_used), len(n_used), used, earlier, axes
            ),
            out_shape=jax.ShapeDtypeStruct(mask.shape + (LAGS,), jnp.float32),
            in_specs=[WHOLE] * (len(arrays) + len(done) + 3),
            scratch_shapes=[lhs, pltpu.VMEM((mask.size, LAGS), jnp.float32)],
            **settings,
        )(*arrays, *done, inner, outer, mask)


def as_rows(block):
    _, windows, parts, bins = block.shape
    block = block.reshape(windows, parts, bins // LANES, LANES)
    return jnp.swapaxes(block, 1, 2).reshape(windows * parts * bins // LANES, LANES)


def two_way(size):
    return size & (size - 1) == 0


def partner(size, k):
    return [(i, i ^ k if two_way(size) else (i + k) % size) for i in range(size)]


def send(block, axis, size, k):
    return lax.ppermute(block, axis, partner(size, k))


def gather(block, axis, size):
    return [block] + [send(block, axis, size, k) for k in range(1, size)]


def gather_by_bits(block, axis, size):
    blocks, bit = {0: block}, size // 2
    while bit:
        for k in list(blocks):
            blocks[k | bit] = send(blocks[k], axis, size, bit)
        bit //= 2
    return [blocks[k] for k in range(size)]


def place(axis, size):
    if axis is None:
        return lambda k: k
    me = lax.axis_index(axis)
    if two_way(size):
        return lambda k: me ^ k
    return lambda k: lax.rem(me + size - k, size)


SMALL = 8


def body(sizes, z_spectra, n_spectra, z_flags, n_flags, pair_mask):
    return steps(sizes, z_spectra, n_spectra, z_flags, n_flags, pair_mask)


def steps(sizes, z_spectra, n_spectra, z_flags, n_flags, pair_mask):
    windows, bins = z_spectra.shape[1], z_spectra.shape[-1]
    rows, cols = sizes
    blank = opening()
    z_own = pack(as_rows(z_spectra), z_flags, blank)
    n_own = pack(as_rows(n_spectra), n_flags, blank)
    inner = prepare(bins, LAGS)
    z_blocks = gather_by_bits(z_own, "col", cols)
    if rows <= SMALL:
        n_blocks = gather(n_own, "row", rows)
        stages = STAGES if sizes == (4, 4) else ((0,) * cols, (0,) * rows)
        return correlate(
            ("col", "row"), stages, z_blocks, n_blocks, pair_mask, inner, windows, bins
        )
    n_all = lax.all_gather(n_own, "row", axis=0)
    step = math.gcd(rows, 4)
    count = rows // step
    stages = ((0,) * cols, (0,) * step)

    def one(args):
        blocks, mask = args
        return correlate(("col", None), stages, z_blocks, list(blocks), mask, inner, windows, bins)

    stacks = lax.map(
        one,
        (
            n_all.reshape((count, step) + n_own.shape),
            jnp.moveaxis(pair_mask.reshape(-1, count, step), 1, 0),
        ),
    )
    return jnp.moveaxis(stacks, 0, 1).reshape(cols, rows, LAGS)


def solution(mesh):
    placed = (
        P(("grp", "row", "col"), None, None, None),
        P(("grp", "col", "row"), None, None, None),
        P(("grp", "row", "col"), None),
        P(("grp", "col", "row"), None),
        P(("grp", "row"), "col"),
    )
    sizes = (mesh.shape["row"], mesh.shape["col"])
    return jax.shard_map(
        functools.partial(body, sizes),
        mesh=mesh,
        in_specs=placed,
        out_specs=P(("grp", "row"), "col", None),
        check_vma=False,
    )
```

time: 22.8 us -> 16.4 us (0.72)
  starting transfers between devices: 15.8 us -> 7.89 us
  waiting for transfers between devices: 3.23 us -> 5.2 us
  local copies, waits for them, and re-layouts: 1.7 us -> 0.86 us
  Pallas kernels: 1.75 us -> 2.19 us
    ppermute x12 -> x6, starting transfers between devices: 15.8 us -> 7.89 us  [send(): return lax.ppermute(block, axis, partner(size, k))]
    ppermute x12 -> x6, waiting for transfers between devices: 3.23 us -> 5.2 us  [send(): return lax.ppermute(block, axis, partner(size, k))]
    unnamed x16, local copies, waits for them, and re-layouts: 1.7 us -> 0.86 us
    pallas_call x2 -> x6, Pallas kernels: 1.75 us -> 2.19 us  [the longest x1 1.08 us: correlate(): pl.pallas_call(functools.partial(last_kernel, shape, LAGS, len(z_used), l...]
  transfers between devices with their start and end apart: 12 -> 6, of which waited for: 3 -> 2; matrix products, arithmetic and copies ran while one was open for 0% -> 0% of each run, Pallas kernels for 1% -> 6%
where the time goes in v2:
time: 16.4 us; the launch traced here: 16.2 us
  starting transfers between devices  7.89 us (48%)
  waiting for transfers between devices  5.2 us (32%)
  Pallas kernels  2.19 us (13%)
  local copies, waits for them, and re-layouts  0.86 us (5%)
    ppermute x6, starting transfers between devices, send(): return lax.ppermute(block, axis, partner(size, k))  7.89 us
    ppermute x6, waiting for transfers between devices, send(): return lax.ppermute(block, axis, partner(size, k))  5.2 us
    pallas_call x1, Pallas kernels, correlate(): pl.pallas_call(functools.partial(last_kernel, shape, LAGS, len(z_used), l...  1.08 us
    unnamed x16, local copies, waits for them, and re-layouts  0.86 us
    pallas_call x1, Pallas kernels, correlate(): pl.pallas_call(functools.partial(stage_kernel, shape, LAGS, len(z_used),...  0.77 us
  transfers between devices with their start and end apart: 6, of which 2 were waited for; matrix products, arithmetic and copies ran while one was open for 0% of the time, Pallas kernels for 6%

profile of v2, /device:TPU:0, one launch (start us, length us, event | category | flops | bytes accessed | tf_op | source)
XLA Modules:
  0.0 16.2 jit_solution(17915370480714053055)
XLA Ops:
  0.0 0.0 copy-start.3
  0.0 0.0 copy-start.6
  0.0 0.8 %copy-done.3 = f32[1,2,2,4096]{3,2,1,0:T(2,128)S(1)} copy-done((f32[1,2,2,4096]{3,2,1,0:T(2,128)S(1)}, f32[1,2,2,4096]{3,2,1,0:T(2,128)}, u32[]{:S(2)}) %copy-start.3) | copy-done | bytes 65560
  0.8 0.0 copy-done.6
  0.8 0.0 copy-start.4
  0.8 0.1 shard_map.83.refs_0_
  0.9 0.0 copy-start.7
  0.9 3.0 %collective-permute-start = (f32[136,128]{1,0:T(8,128)S(1)}, f32[136,128]{1,0:T(8,128)S(1)}, u32[]{:S(2)}, u32[]{:S(2)}) collective-permute-start(f32[136,128]{1,0:T(8,128)S(1)} %shard_map.83.refs_0_), channel_id=1, source_target_pairs={{0,2},{1,3},{2,0},{3,1},{4,6},{5,7},{6,4},{7,5},{8,10},{9,11},{10,... | collective-permute-start | bytes 208904 | tf_op jit(solution)/shard_map/ppermute | solution.py:237
  3.9 0.0 copy-done.4
  3.9 0.0 copy-done.7
  3.9 0.0 copy-start.1
  3.9 0.0 copy-start.2
  3.9 0.1 shard_map.84.refs_3_.refs_1_
  4.0 1.6 %collective-permute-start.2 = (f32[136,128]{1,0:T(8,128)S(1)}, f32[136,128]{1,0:T(8,128)S(1)}, u32[]{:S(2)}, u32[]{:S(2)}) collective-permute-start(f32[136,128]{1,0:T(8,128)S(1)} %shard_map.84.refs_3_.refs_1_), channel_id=1, source_target_pairs={{0,4},{4,0},{8,12},{12,8},{1,5},{5,1},{9,13},{13,9},{2,6},{6,2},{1... | collective-permute-start | bytes 208904 | tf_op jit(solution)/shard_map/ppermute | solution.py:237
  5.6 2.6 %collective-permute-start.3 = (f32[136,128]{1,0:T(8,128)S(1)}, f32[136,128]{1,0:T(8,128)S(1)}, u32[]{:S(2)}, u32[]{:S(2)}) collective-permute-start(f32[136,128]{1,0:T(8,128)S(1)} %shard_map.84.refs_3_.refs_1_), channel_id=1, source_target_pairs={{0,8},{4,12},{8,0},{12,4},{1,9},{5,13},{9,1},{13,5},{2,10},{6,14},... | collective-permute-start | bytes 208904 | tf_op jit(solution)/shard_map/ppermute | solution.py:237
  8.2 0.2 %collective-permute-start.4 = (f32[136,128]{1,0:T(8,128)S(1)}, f32[136,128]{1,0:T(8,128)S(1)}, u32[]{:S(2)}, u32[]{:S(2)}) collective-permute-start(f32[136,128]{1,0:T(8,128)S(1)} %shard_map.84.refs_3_.refs_1_), channel_id=1, source_target_pairs={{0,12},{4,8},{8,4},{12,0},{1,13},{5,9},{9,5},{13,1},{2,14},{6,10},... | collective-permute-start | bytes 208904 | tf_op jit(solution)/shard_map/ppermute | solution.py:237
  8.4 0.0 collective-permute-start.5
  8.4 0.0 collective-permute-done.refs_2_
  8.4 0.5 %collective-permute-start.1 = (f32[136,128]{1,0:T(8,128)S(1)}, f32[136,128]{1,0:T(8,128)S(1)}, u32[]{:S(2)}, u32[]{:S(2)}) collective-permute-start(f32[136,128]{1,0:T(8,128)S(1)} %collective-permute-done.refs_2_), channel_id=1, source_target_pairs={{0,1},{1,0},{2,3},{3,2},{4,5},{5,4},{6,7},{7,6},{8,9},{9,8},{10,11... | collective-permute-start | bytes 208904 | tf_op jit(solution)/shard_map/ppermute | solution.py:237
  8.9 0.0 copy-done.1
  8.9 0.0 copy-done.2
  8.9 0.2 %shard_map.85.refs_7_.refs_6_ = bf16[512,1024]{1,0:T(8,128)(2,1)S(1)} custom-call(f32[16,1024]{1,0:T(8,128)S(1)} %copy-done.1, f32[16,1024]{1,0:T(8,128)S(1)} %copy-done.2), custom_call_target="tpu_custom_call" | custom-call | flops 8388608 | bytes 1048576 | tf_op jit(solution)/shard_map/pallas_call | solution.py:87
  9.1 0.0 copy-start.5
  9.1 0.0 collective-permute-done.2.refs_4_.refs_2_
  9.1 3.7 %collective-permute-done.3.refs_5_.refs_3_ = f32[136,128]{1,0:T(8,128)S(1)} collective-permute-done((f32[136,128]{1,0:T(8,128)S(1)}, f32[136,128]{1,0:T(8,128)S(1)}, u32[]{:S(2)}, u32[]{:S(2)}) %collective-permute-start.3) | collective-permute-done | bytes 69664 | tf_op jit(solution)/shard_map/ppermute | solution.py:237
  12.8 1.5 %collective-permute-done.4.refs_6_.refs_4_ = f32[136,128]{1,0:T(8,128)S(1)} collective-permute-done((f32[136,128]{1,0:T(8,128)S(1)}, f32[136,128]{1,0:T(8,128)S(1)}, u32[]{:S(2)}, u32[]{:S(2)}) %collective-permute-start.4) | collective-permute-done | bytes 69664 | tf_op jit(solution)/shard_map/ppermute | solution.py:237
  14.3 0.0 collective-permute-done.5.refs_1_
  14.3 0.0 copy-done
  14.3 0.8 %shard_map.86.refs_5_ = f32[12,512]{1,0:T(8,128)S(1)} custom-call(f32[136,128]{1,0:T(8,128)S(1)} %shard_map.83.refs_0_, f32[136,128]{1,0:T(8,128)S(1)} %collective-permute-done.5.refs_1_, f32[136,128]{1,0:T(8,128)S(1)} %collective-permute-done.refs_2_, f32[136,128]{1,0:T(8,128)S(1)} %shard_map.84.refs_3_.refs_1_, ...), custom_call_target="tpu_custom_call" | custom-call | flops 402653184 | bytes 786432 | tf_op jit(solution)/shard_map/pallas_call | solution.py:200
  15.1 0.0 collective-permute-done.1.refs_0_
  15.1 0.0 copy-done.5
  15.1 1.1 %shard_map.87 = f32[4,4,512]{2,1,0:T(4,128)} custom-call(f32[136,128]{1,0:T(8,128)S(1)} %collective-permute-done.1.refs_0_, f32[136,128]{1,0:T(8,128)S(1)} %shard_map.84.refs_3_.refs_1_, f32[136,128]{1,0:T(8,128)S(1)} %collective-permute-done.2.refs_4_.refs_2_, f32[136,128]{1,0:T(8,128)S(1)} %collective-permute-done.3.refs_5_.refs_3_, ...), custom_call_target="tpu_custom_call" | custom-call | flops 134217728 | bytes 262144 | tf_op jit(solution)/shard_map/pallas_call | solution.py:211
  (2 shorter events, 0.0 us)
Async XLA Ops:
  0.0 0.8 %copy-start.3 = (f32[1,2,2,4096]{3,2,1,0:T(2,128)S(1)}, f32[1,2,2,4096]{3,2,1,0:T(2,128)}, u32[]{:S(2)}) copy-start(f32[1,2,2,4096]{3,2,1,0:T(2,128)} %param.8) | copy-start | bytes 196612
  0.0 0.8 %copy-start.6 = (s32[1,2]{1,0:T(1,128)S(1)}, s32[1,2]{1,0:T(1,128)}, u32[]{:S(2)}) copy-start(s32[1,2]{1,0:T(1,128)} %flag_ref.2) | copy-start | bytes 28
  0.8 3.1 %copy-start.4 = (f32[1,2,2,4096]{3,2,1,0:T(2,128)S(1)}, f32[1,2,2,4096]{3,2,1,0:T(2,128)}, u32[]{:S(2)}) copy-start(f32[1,2,2,4096]{3,2,1,0:T(2,128)} %param.9) | copy-start | bytes 196612
  0.9 3.0 %copy-start.7 = (s32[1,2]{1,0:T(1,128)S(1)}, s32[1,2]{1,0:T(1,128)}, u32[]{:S(2)}) copy-start(s32[1,2]{1,0:T(1,128)} %flag_ref.3) | copy-start | bytes 28
  0.9 7.5 %collective-permute-start = (f32[136,128]{1,0:T(8,128)S(1)}, f32[136,128]{1,0:T(8,128)S(1)}, u32[]{:S(2)}, u32[]{:S(2)}) collective-permute-start(f32[136,128]{1,0:T(8,128)S(1)} %shard_map.83.refs_0_), channel_id=1, source_target_pairs={{0,2},{1,3},{2,0},{3,1},{4,6},{5,7},{6,4},{7,5},{8,10},{9,11},{10,... | collective-permute-start | bytes 208904 | tf_op jit(solution)/shard_map/ppermute | solution.py:237
  3.9 5.0 %copy-start.1 = (f32[16,1024]{1,0:T(8,128)S(1)}, f32[16,1024]{1,0:T(8,128)}, u32[]{:S(2)}) copy-start(f32[16,1024]{1,0:T(8,128)} %constant.6.clone.coarse_ref) | copy-start | bytes 196612
  3.9 5.0 %copy-start.2 = (f32[16,1024]{1,0:T(8,128)S(1)}, f32[16,1024]{1,0:T(8,128)}, u32[]{:S(2)}) copy-start(f32[16,1024]{1,0:T(8,128)} %constant.7.clone.fine_ref) | copy-start | bytes 196612
  4.0 10.3 %copy-start = (f32[16,1024]{1,0:T(8,128)S(1)}, f32[16,1024]{1,0:T(8,128)}, u32[]{:S(2)}) copy-start(f32[16,1024]{1,0:T(8,128)} %constant.8.clone.refs_8_.refs_7_) | copy-start | bytes 196612
  4.0 5.1 %collective-permute-start.2 = (f32[136,128]{1,0:T(8,128)S(1)}, f32[136,128]{1,0:T(8,128)S(1)}, u32[]{:S(2)}, u32[]{:S(2)}) collective-permute-start(f32[136,128]{1,0:T(8,128)S(1)} %shard_map.84.refs_3_.refs_1_), channel_id=1, source_target_pairs={{0,4},{4,0},{8,12},{12,8},{1,5},{5,1},{9,13},{13,9},{2,6},{6,2},{1... | collective-permute-start | bytes 208904 | tf_op jit(solution)/shard_map/ppermute | solution.py:237
  5.6 7.2 %collective-permute-start.3 = (f32[136,128]{1,0:T(8,128)S(1)}, f32[136,128]{1,0:T(8,128)S(1)}, u32[]{:S(2)}, u32[]{:S(2)}) collective-permute-start(f32[136,128]{1,0:T(8,128)S(1)} %shard_map.84.refs_3_.refs_1_), channel_id=1, source_target_pairs={{0,8},{4,12},{8,0},{12,4},{1,9},{5,13},{9,1},{13,5},{2,10},{6,14},... | collective-permute-start | bytes 208904 | tf_op jit(solution)/shard_map/ppermute | solution.py:237
  8.2 6.1 %collective-permute-start.4 = (f32[136,128]{1,0:T(8,128)S(1)}, f32[136,128]{1,0:T(8,128)S(1)}, u32[]{:S(2)}, u32[]{:S(2)}) collective-permute-start(f32[136,128]{1,0:T(8,128)S(1)} %shard_map.84.refs_3_.refs_1_), channel_id=1, source_target_pairs={{0,12},{4,8},{8,4},{12,0},{1,13},{5,9},{9,5},{13,1},{2,14},{6,10},... | collective-permute-start | bytes 208904 | tf_op jit(solution)/shard_map/ppermute | solution.py:237
  8.4 5.9 %collective-permute-start.5 = (f32[136,128]{1,0:T(8,128)S(1)}, f32[136,128]{1,0:T(8,128)S(1)}, u32[]{:S(2)}, u32[]{:S(2)}) collective-permute-start(f32[136,128]{1,0:T(8,128)S(1)} %shard_map.83.refs_0_), channel_id=1, source_target_pairs={{0,1},{1,0},{2,3},{3,2},{4,5},{5,4},{6,7},{7,6},{8,9},{9,8},{10,11... | collective-permute-start | bytes 208904 | tf_op jit(solution)/shard_map/ppermute | solution.py:237
  8.4 6.7 %collective-permute-start.1 = (f32[136,128]{1,0:T(8,128)S(1)}, f32[136,128]{1,0:T(8,128)S(1)}, u32[]{:S(2)}, u32[]{:S(2)}) collective-permute-start(f32[136,128]{1,0:T(8,128)S(1)} %collective-permute-done.refs_2_), channel_id=1, source_target_pairs={{0,1},{1,0},{2,3},{3,2},{4,5},{5,4},{6,7},{7,6},{8,9},{9,8},{10,11... | collective-permute-start | bytes 208904 | tf_op jit(solution)/shard_map/ppermute | solution.py:237
  9.1 6.0 %copy-start.5 = (s32[4,4]{1,0:T(4,128)S(1)}, s32[4,4]{1,0:T(4,128)}, u32[]{:S(2)}) copy-start(s32[4,4]{1,0:T(4,128)} %refs_8_.2) | copy-start | bytes 196
